TPU v7x, 256 devices: a whole 4x4x8 slice. The times are simulated.
256 devices in a mesh: gx: 8 (over y, core), gy: 32 (over z, x).
Axes of the slice: x: 4, y: 4, z: 8, core: 2. Of those that a mesh axis runs over, the one named last changes fastest.
Arguments:
- pressure: float32 [512, 512, 512], P('gx', 'gy'), may hold values from -6 to 6
- divergence: float32 [512, 512, 512], P('gx', 'gy'), may hold values from -6 to 6
- diagonal: float32 [512, 512, 512], P('gx', 'gy'), may hold values from 0.05 to 0.5
- normals: float32 [3, 262144], P(None, ('gx', 'gy')), may hold values from -6 to 6
- traction: float32 [3, 262144], P(None, ('gx', 'gy')), may hold values from -3 to 3
- slot_of: int32 [8, 32768], P('gx'), may hold values from 0 to 98303, as said below
- counts: int32 [256], P(('gx', 'gy')), may hold values from 0 to 3072, as said below
- previous: float32 [3, 786432], P(None, ('gx', 'gy')), may hold values from -6 to 6
- secant_v: float32 [32, 3, 786432], P(None, None, ('gx', 'gy')), may hold values from -6 to 6
- secant_w: float32 [32, 3, 786432], P(None, None, ('gx', 'gy')), may hold values from -940.60406 to 940.60406
Outputs:
- pressure_new: float32 [512, 512, 512], P('gx', 'gy')
- coupled: float32 [3, 786432], P(None, ('gx', 'gy'))
Inputs may be any that keep to these rules, and one draw needn't show every extreme that they name: Within each group (row of slot_of) the places are distinct; place o * 3072 + s has s < counts[a * 32 + o]; every such place is used; the rows of one device (aligned blocks of 1024 entries) send at most 96 rows to one owner, and exactly 96 to some owner. The counts of one group sum to 32768; some owner of every group holds exactly 3072.
All inputs are finite; a program needn't handle non-finite values.
Results may differ from a plain program's by a relative error of at most 0.00019.
Values sent between devices are 32-bit elements; how exact they have to be, the bound alone decides.
A program may use at most 128 MiB of HBM per device.

v0:
```python
import jax
import jax.numpy as jnp
from jax import lax
from jax.sharding import PartitionSpec as P

SWEEPS = 2


def extended(cells, sides, width):
    for axis, dim in sides:
        count = lax.axis_size(axis)
        ends = count - 1
        head = lax.slice_in_dim(cells, 0, width, axis=dim)
        tail = lax.slice_in_dim(cells, cells.shape[dim] - width, cells.shape[dim], axis=dim)
        cells = jnp.concatenate(
            [
                lax.ppermute(tail, axis, [(i, (i + 1) % count) for i in range(ends)]),
                cells,
                lax.ppermute(head, axis, [((i + 1) % count, i) for i in range(ends)]),
            ],
            axis=dim,
        )
    return cells


def stencil_sum(padded):
    padded = jnp.pad(padded, ((0, 0), (0, 0), (1, 1)))
    total = padded[2:, 1:-1, 1:-1] + padded[:-2, 1:-1, 1:-1]
    total = total + padded[1:-1, 2:, 1:-1] + padded[1:-1, :-2, 1:-1]
    total = total + padded[1:-1, 1:-1, 2:] + padded[1:-1, 1:-1, :-2]
    return total


def sweep_once(field, divergence, diagonal):
    padded = extended(field, (("gx", 0), ("gy", 1)), 1)
    return (divergence + stencil_sum(padded)) / (6.0 + diagonal)


def shards(
    pressure, divergence, diagonal, normals, traction, slot_of, counts, previous, secant_v, secant_w
):
    columns = secant_v.shape[0]
    capacity = previous.shape[1]
    slot_index = jnp.arange(capacity, dtype=jnp.int32)
    occupied = (slot_index < counts[0]).astype(jnp.float32)
    masked_v = (secant_v * occupied[None, None, :]).reshape(columns, 3 * capacity)
    gram_local = jnp.dot(masked_v, masked_v.T, precision=lax.Precision.HIGHEST)
    field = pressure
    for sweep_index in range(SWEEPS):
        field = sweep_once(field, divergence, diagonal)
    surface = field[:, :, -1].reshape(-1)
    forces = normals * surface[None, :] + traction
    own_index = lax.axis_index("gy")
    all_slots = slot_of[0]
    gathered = lax.all_gather(forces, "gy", axis=1, tiled=True)
    placed = jnp.where(all_slots // capacity == own_index, all_slots % capacity, capacity)
    owned = jnp.zeros((3, capacity), jnp.float32).at[:, placed].set(gathered, mode="drop")
    residual = occupied[None, :] * (owned - previous)
    projection_local = jnp.dot(
        masked_v, residual.reshape(3 * capacity), precision=lax.Precision.HIGHEST
    )
    gram, projection = lax.psum((gram_local, projection_local), ("gx", "gy"))
    factor = jnp.linalg.cholesky(gram)
    coefficient = -jax.scipy.linalg.cho_solve((factor, True), projection)
    update = jnp.dot(
        coefficient, secant_w.reshape(columns, 3 * capacity), precision=lax.Precision.HIGHEST
    ).reshape(3, capacity)
    coupled = occupied[None, :] * (owned + update)
    return (field, coupled)


def solution(mesh):
    placed = (
        P("gx", "gy", None),
        P("gx", "gy", None),
        P("gx", "gy", None),
        P(None, ("gx", "gy")),
        P(None, ("gx", "gy")),
        P("gx", None),
        P(("gx", "gy")),
        P(None, ("gx", "gy")),
        P(None, None, ("gx", "gy")),
        P(None, None, ("gx", "gy")),
    )
    return jax.shard_map(
        shards,
        mesh=mesh,
        in_specs=placed,
        out_specs=(P("gx", "gy", None), P(None, ("gx", "gy"))),
        check_vma=False,
    )
```

profile of v0, /device:TPU:1, one launch (start us, length us, event | category | flops | bytes accessed | tf_op | source)
XLA Modules:
  0.0 306.0 jit_solution(7569810159518206231)
XLA Ops:
  0.6 0.0 copy-start
  0.6 0.9 fusion.35
  1.6 5.1 %collective-permute-start = (f32[1,16,512]{2,0,1:T(1,128)S(1)}, f32[1,16,512]{2,0,1:T(1,128)S(1)}, u32[]{:S(2)}, u32[]{:S(2)}) collective-permute-start(f32[1,16,512]{2,0,1:T(1,128)S(1)} %copy.23), channel_id=1, source_target_pairs={{32,0},{64,32},{96,64},{128,96},{160,128},{192,160},{224,192},{33,... | collective-permute-start | bytes 98312 | tf_op jit(solution)/shard_map/ppermute | solution.py:19
  6.7 1.9 collective-permute-start.1
  8.6 2.8 copy.24
  11.5 0.0 copy-start.1
  11.5 0.0 copy-start.7
  11.5 0.0 collective-permute-done
  11.5 0.0 collective-permute-done.1
  11.6 1.4 collective-permute-start.2
  13.0 4.0 %collective-permute-start.3 = (f32[66,1,512]{2,0,1:T(8,128)S(1)}, f32[66,1,512]{2,0,1:T(8,128)S(1)}, u32[]{:S(2)}, u32[]{:S(2)}) collective-permute-start(f32[66,1,512]{2,0,1:T(8,128)S(1)} %get-tuple-element.12), channel_id=1, source_target_pairs={{0,1},{1,2},{2,3},{3,4},{4,5},{5,6},{6,7},{7,8},{8,9},{9,10},{10,1... | collective-permute-start | bytes 405512 | tf_op jit(solution)/shard_map/ppermute | solution.py:17
  17.0 0.0 copy-done.7
  17.0 1.8 compare_select_fusion
  19.4 0.0 copy-start.2
  19.5 0.0 copy-start.4
  19.5 0.0 collective-permute-done.2
  19.5 0.0 collective-permute-done.3
  19.5 0.0 copy-done.1
  19.5 2.8 select_maximum_fusion.4
  22.3 0.0 copy-done.2
  22.4 0.0 copy-done.4
  22.4 0.0 copy-start.8
  22.4 6.9 %fusion.7 = f32[64,16,512]{2,0,1:T(8,128)S(1)} fusion(f32[66,18,514]{2,0,1:T(8,128)S(1)} %select_maximum_fusion.4, f32[66,1,512]{2,0,1:T(8,128)S(1)} %collective-permute-done.3, f32[1,16,512]{2,0,1:T(1,128)S(1)} %collective-permute-done, f32[64,16,512]{2,0,1:T(8,128)} %copy-done.1, f32[1,16,512]{2,0,1:T(1,128)S(1)} %collective-permute-done.1, ...), kind=kLoop, calls=%fused_computation.29 | loop fusion | flops 8388608 | bytes 12918784 | tf_op jit(solution)/shard_map/div | solution.py:36
  29.3 0.1 fusion.34
  29.3 3.4 %collective-permute-start.4 = (f32[1,16,512]{2,0,1:T(1,128)S(1)}, f32[1,16,512]{2,0,1:T(1,128)S(1)}, u32[]{:S(2)}, u32[]{:S(2)}) collective-permute-start(f32[1,16,512]{2,0,1:T(1,128)S(1)} %get-tuple-element.15), channel_id=1, source_target_pairs={{32,0},{64,32},{96,64},{128,96},{160,128},{192,160},{224,192},{33,... | collective-permute-start | bytes 98312 | tf_op jit(solution)/shard_map/ppermute | solution.py:19
  32.8 2.6 collective-permute-start.5
  35.4 0.0 copy-done.8
  35.4 1.7 copy.35
  37.0 0.0 collective-permute-done.4
  37.1 0.0 collective-permute-done.5
  37.1 1.4 collective-permute-start.6
  38.5 4.9 %collective-permute-start.7 = (f32[66,1,512]{2,0,1:T(8,128)S(1)}, f32[66,1,512]{2,0,1:T(8,128)S(1)}, u32[]{:S(2)}, u32[]{:S(2)}) collective-permute-start(f32[66,1,512]{2,0,1:T(8,128)S(1)} %get-tuple-element.10), channel_id=1, source_target_pairs={{0,1},{1,2},{2,3},{3,4},{4,5},{5,6},{6,7},{7,8},{8,9},{9,10},{10,1... | collective-permute-start | bytes 405512 | tf_op jit(solution)/shard_map/ppermute | solution.py:17
  43.5 1.1 convolution_bitcast_fusion
  44.5 0.0 copy-start.3
  44.6 0.0 copy-start.5
  44.6 1.1 collective-permute-done.6
  45.7 0.9 collective-permute-done.7
  46.6 2.8 select_maximum_fusion
  49.5 6.7 %fusion.2 = f32[64,16,512]{2,0,1:T(8,128)S(1)} fusion(f32[66,18,514]{2,0,1:T(8,128)S(1)} %select_maximum_fusion, f32[66,1,512]{2,0,1:T(8,128)S(1)} %collective-permute-done.7, f32[1,16,512]{2,0,1:T(1,128)S(1)} %collective-permute-done.4, f32[64,16,512]{2,0,1:T(8,128)S(1)} %fusion.7, f32[1,16,512]{2,0,1:T(1,128)S(1)} %collective-permute-done.5, ...), kind=kLoop, calls=%fused_computation.14 | loop fusion | flops 8388608 | bytes 12918784 | tf_op jit(solution)/shard_map/div | solution.py:36
  56.2 0.2 slice.128
  56.4 0.0 copy-start.10
  56.4 2.5 copy.37
  59.0 0.5 copy.31
  59.5 0.1 mul.33
  59.5 0.0 copy-done.9
  59.5 0.0 copy-done.10
  59.6 48.0 %all_gather.3 = f32[3,32768]{1,0:T(4,128)S(1)} all-gather(f32[3,1024]{1,0:T(4,128)S(1)} %multiply_add_fusion), channel_id=1, replica_groups=mesh['gx'=8,'gy'=32] {'gy'}, dimensions={1}, use_global_device_ids=true | all-gather | bytes 405504 | tf_op jit(solution)/shard_map/all_gather | solution.py:55
  107.6 8.5 %copy.32 = f32[32768,3]{1,0:T(8,128)} copy(f32[32768,3]{0,1:T(4,128)S(1)} %bitcast.77) | data formatting | bytes 786432 | tf_op jit(solution)/shard_map/all_gather | solution.py:55
  116.1 80.8 %scatter_custom_fusion = f32[3,3072]{0,1:T(8,128)S(1)} fusion(s32[32768]{0:T(1024)} %bitcast.78, f32[32768,3]{1,0:T(8,128)} %copy.32, f32[]{:T(128)} %constant.70.clone.1), kind=kCustom, calls=%fused_computation.58 | custom fusion | bytes 37376 | tf_op jit(solution)/shard_map/scatter | solution.py:57
  196.9 3.0 multiply_bitcast_fusion
  200.0 1.9 copy.40
  201.8 2.3 fusion.20
  204.1 86.8 %all-reduce.2 = (f32[32,32]{0,1:T(8,128)S(1)}, f32[32]{0:T(128)S(1)}) all-reduce(f32[32,32]{0,1:T(8,128)S(1)} %convolution_bitcast_fusion, f32[32]{0:T(128)S(1)} %fusion.20), channel_id=1, replica_groups=mesh['gx'=8,'gy'=32] {'gx','gy'}, use_global_device_ids=true, to_apply=%region_1.2 | all-reduce | flops 1056 | bytes 8448 | tf_op jit(solution)/shard_map/psum | solution.py:62
  291.0 0.1 copy.34
  291.1 2.9 cholesky.16
  294.0 0.6 compare_reduce_fusion
  294.7 0.7 fusion.28
  295.3 2.4 custom-call.10
  297.7 0.2 convolution_bitcast_fusion.2
  297.9 0.1 fusion.19
  298.1 0.7 fusion.12
  298.7 1.7 copy.42
  300.4 3.0 fusion.11
  303.5 2.5 copy.38
  (14 shorter events, 0.2 us)
Async XLA Ops:
  0.6 297.4 %copy-start = (f32[32,3,3072]{2,0,1:T(8,128)S(1)}, f32[32,3,3072]{2,0,1:T(8,128)}, u32[]{:S(2)}) copy-start(f32[32,3,3072]{2,0,1:T(8,128)} %param.19) | copy-start | bytes 3538948
  1.6 9.9 %collective-permute-start = (f32[1,16,512]{2,0,1:T(1,128)S(1)}, f32[1,16,512]{2,0,1:T(1,128)S(1)}, u32[]{:S(2)}, u32[]{:S(2)}) collective-permute-start(f32[1,16,512]{2,0,1:T(1,128)S(1)} %copy.23), channel_id=1, source_target_pairs={{32,0},{64,32},{96,64},{128,96},{160,128},{192,160},{224,192},{33,... | collective-permute-start | bytes 98312 | tf_op jit(solution)/shard_map/ppermute | solution.py:19
  6.7 4.8 %collective-permute-start.1 = (f32[1,16,512]{2,0,1:T(1,128)S(1)}, f32[1,16,512]{2,0,1:T(1,128)S(1)}, u32[]{:S(2)}, u32[]{:S(2)}) collective-permute-start(f32[1,16,512]{2,0,1:T(1,128)S(1)} %copy.25), channel_id=1, source_target_pairs={{0,32},{32,64},{64,96},{96,128},{128,160},{160,192},{192,224},{1,3... | collective-permute-start | bytes 98312 | tf_op jit(solution)/shard_map/ppermute | solution.py:17
  11.5 8.0 %copy-start.1 = (f32[64,16,512]{2,0,1:T(8,128)}, f32[64,16,512]{2,0,1:T(8,128)S(1)}, u32[]{:S(2)}) copy-start(f32[64,16,512]{2,0,1:T(8,128)S(1)} %copy.24) | copy-start | bytes 6291460
  11.5 5.5 %copy-start.7 = (s32[1,32768]{1,0:T(1,128)S(1)}, s32[1,32768]{1,0:T(1,128)}, u32[]{:S(2)}) copy-start(s32[1,32768]{1,0:T(1,128)} %param.15) | copy-start | bytes 393220
  11.6 7.9 %collective-permute-start.2 = (f32[66,1,512]{2,0,1:T(8,128)S(1)}, f32[66,1,512]{2,0,1:T(8,128)S(1)}, u32[]{:S(2)}, u32[]{:S(2)}) collective-permute-start(f32[66,1,512]{2,0,1:T(8,128)S(1)} %get-tuple-element.13), channel_id=1, source_target_pairs={{1,0},{2,1},{3,2},{4,3},{5,4},{6,5},{7,6},{8,7},{9,8},{10,9},{11,1... | collective-permute-start | bytes 405512 | tf_op jit(solution)/shard_map/ppermute | solution.py:19
  13.0 6.5 %collective-permute-start.3 = (f32[66,1,512]{2,0,1:T(8,128)S(1)}, f32[66,1,512]{2,0,1:T(8,128)S(1)}, u32[]{:S(2)}, u32[]{:S(2)}) collective-permute-start(f32[66,1,512]{2,0,1:T(8,128)S(1)} %get-tuple-element.12), channel_id=1, source_target_pairs={{0,1},{1,2},{2,3},{3,4},{4,5},{5,6},{6,7},{7,8},{8,9},{9,10},{10,1... | collective-permute-start | bytes 405512 | tf_op jit(solution)/shard_map/ppermute | solution.py:17
  19.4 2.9 copy-start.2
  19.5 2.9 copy-start.4
  22.4 13.0 %copy-start.8 = (f32[3,3072]{1,0:T(4,128)S(1)}, f32[3,3072]{1,0:T(4,128)}, u32[]{:S(2)}) copy-start(f32[3,3072]{1,0:T(4,128)} %param.17) | copy-start | bytes 110596
  29.3 7.7 %collective-permute-start.4 = (f32[1,16,512]{2,0,1:T(1,128)S(1)}, f32[1,16,512]{2,0,1:T(1,128)S(1)}, u32[]{:S(2)}, u32[]{:S(2)}) collective-permute-start(f32[1,16,512]{2,0,1:T(1,128)S(1)} %get-tuple-element.15), channel_id=1, source_target_pairs={{32,0},{64,32},{96,64},{128,96},{160,128},{192,160},{224,192},{33,... | collective-permute-start | bytes 98312 | tf_op jit(solution)/shard_map/ppermute | solution.py:19
  32.8 4.3 %collective-permute-start.5 = (f32[1,16,512]{2,0,1:T(1,128)S(1)}, f32[1,16,512]{2,0,1:T(1,128)S(1)}, u32[]{:S(2)}, u32[]{:S(2)}) collective-permute-start(f32[1,16,512]{2,0,1:T(1,128)S(1)} %get-tuple-element.14), channel_id=1, source_target_pairs={{0,32},{32,64},{64,96},{96,128},{128,160},{160,192},{192,224},{1,3... | collective-permute-start | bytes 98312 | tf_op jit(solution)/shard_map/ppermute | solution.py:17
  37.0 6.4 %copy-start.6 = (f32[32,3,3072]{2,0,1:T(8,128)S(1)}, f32[32,3,3072]{2,0,1:T(8,128)}, u32[]{:S(2)}) copy-start(f32[32,3,3072]{2,0,1:T(8,128)} %param.18) | copy-start | bytes 3538948
  37.1 8.6 %collective-permute-start.6 = (f32[66,1,512]{2,0,1:T(8,128)S(1)}, f32[66,1,512]{2,0,1:T(8,128)S(1)}, u32[]{:S(2)}, u32[]{:S(2)}) collective-permute-start(f32[66,1,512]{2,0,1:T(8,128)S(1)} %get-tuple-element.11), channel_id=1, source_target_pairs={{1,0},{2,1},{3,2},{4,3},{5,4},{6,5},{7,6},{8,7},{9,8},{10,9},{11,1... | collective-permute-start | bytes 405512 | tf_op jit(solution)/shard_map/ppermute | solution.py:19
  38.5 8.1 %collective-permute-start.7 = (f32[66,1,512]{2,0,1:T(8,128)S(1)}, f32[66,1,512]{2,0,1:T(8,128)S(1)}, u32[]{:S(2)}, u32[]{:S(2)}) collective-permute-start(f32[66,1,512]{2,0,1:T(8,128)S(1)} %get-tuple-element.10), channel_id=1, source_target_pairs={{0,1},{1,2},{2,3},{3,4},{4,5},{5,6},{6,7},{7,8},{8,9},{9,10},{10,1... | collective-permute-start | bytes 405512 | tf_op jit(solution)/shard_map/ppermute | solution.py:17
  44.5 4.9 %copy-start.3 = (f32[64,16,512]{2,1,0:T(8,128)S(1)}, f32[64,16,512]{2,1,0:T(8,128)}, u32[]{:S(2)}) copy-start(f32[64,16,512]{2,1,0:T(8,128)} %param.11) | copy-start | bytes 6291460
  44.6 4.9 %copy-start.5 = (f32[64,16,512]{2,1,0:T(8,128)S(1)}, f32[64,16,512]{2,1,0:T(8,128)}, u32[]{:S(2)}) copy-start(f32[64,16,512]{2,1,0:T(8,128)} %param.12) | copy-start | bytes 6291460
  56.4 3.1 %copy-start.9 = (f32[3,1024]{1,0:T(4,128)S(1)}, f32[3,1024]{1,0:T(4,128)}, u32[]{:S(2)}) copy-start(f32[3,1024]{1,0:T(4,128)} %param.14) | copy-start | bytes 36868
  56.4 3.1 %copy-start.10 = (f32[3,1024]{1,0:T(4,128)S(1)}, f32[3,1024]{1,0:T(4,128)}, u32[]{:S(2)}) copy-start(f32[3,1024]{1,0:T(4,128)} %param.13) | copy-start | bytes 36868
where the time goes:
time: 307 us; the launch traced here: 306 us
  blocking collectives  135 us (44%)
  local copies, waits for them, and re-layouts  104 us (34%)
  other arithmetic  33.9 us (11%)
  starting transfers between devices  24.8 us (8%)
  matrix products  4.35 us (1%)
    psum x1, blocking collectives, shards(): gram, projection = lax.psum((gram_local, projection_local), ('gx', 'gy'))  86.8 us
    scatter x1, local copies, waits for them, and re-layouts, shards(): jnp.zeros((3, capacity), jnp.float32).at[:, placed]  80.8 us
    all_gather x1, blocking collectives, shards(): gathered = lax.all_gather(forces, 'gy', axis=1, tiled=True)  48 us
    div x2, other arithmetic, sweep_once(): return (divergence + stencil_sum(padded)) / (6.0 + diagonal)  13.6 us
    ppermute x4, starting transfers between devices, extended(): lax.ppermute(tail, axis, [(i, (i + 1) % count) for i in range(ends)])  13.4 us
    ppermute x4, starting transfers between devices, extended(): lax.ppermute(head, axis, [((i + 1) % count, i) for i in range(ends)])  11.4 us
    unnamed x26, local copies, waits for them, and re-layouts  9.59 us
    all_gather x1, local copies, waits for them, and re-layouts, shards(): gathered = lax.all_gather(forces, 'gy', axis=1, tiled=True)  8.53 us
  transfers between devices with their start and end apart: 8, of which 2 were waited for; matrix products, arithmetic and copies ran while one was open for 2% of the time, Pallas kernels for 0%

commit v1 on v0

--- a/solution.py
+++ b/solution.py
@@ -4,6 +4,11 @@
 from jax.sharding import PartitionSpec as P
 
 SWEEPS = 2
+
+
+def tiled_gather(shard, axis, dim):
+    copies = jnp.concatenate([shard] * lax.axis_size(axis), axis=dim)
+    return lax.all_to_all(copies, axis, dim, dim, tiled=True)
 
 
 def extended(cells, sides, width):
@@ -52,7 +57,7 @@
     forces = normals * surface[None, :] + traction
     own_index = lax.axis_index("gy")
     all_slots = slot_of[0]
-    gathered = lax.all_gather(forces, "gy", axis=1, tiled=True)
+    gathered = tiled_gather(forces, "gy", 1)
     placed = jnp.where(all_slots // capacity == own_index, all_slots % capacity, capacity)
     owned = jnp.zeros((3, capacity), jnp.float32).at[:, placed].set(gathered, mode="drop")
     residual = occupied[None, :] * (owned - previous)

time: 307 us -> 281 us (0.915)
  blocking collectives: 135 us -> 74.8 us
  starting transfers between devices: 24.8 us -> 42.9 us
  waiting for transfers between devices: 2.07 us -> 13.4 us
  local copies, waits for them, and re-layouts: 104 us -> 108 us
    all_gather x1 -> x0, blocking collectives: 48 us -> none  [shards(): gathered = lax.all_gather(forces, 'gy', axis=1, tiled=True)]
    all_to_all x0 -> x1, starting transfers between devices: none -> 17.6 us  [tiled_gather(): return lax.all_to_all(copies, axis, dim, dim, tiled=True)]
    psum x1, blocking collectives: 86.8 us -> 74.8 us  [shards(): gram, projection = lax.psum((gram_local, projection_local), ('gx', 'gy'))]
    all_to_all x0 -> x1, local copies, waits for them, and re-layouts: none -> 9.07 us  [tiled_gather(): return lax.all_to_all(copies, axis, dim, dim, tiled=True)]
    all_gather x1 -> x0, local copies, waits for them, and re-layouts: 8.53 us -> none  [shards(): gathered = lax.all_gather(forces, 'gy', axis=1, tiled=True)]
    all_to_all x0 -> x1, waiting for transfers between devices: none -> 6.87 us  [tiled_gather(): return lax.all_to_all(copies, axis, dim, dim, tiled=True)]
    unnamed x26 -> x56, local copies, waits for them, and re-layouts: 9.59 us -> 12.8 us
  transfers between devices with their start and end apart: 8 -> 9, of which waited for: 2 -> 6; matrix products, arithmetic and copies ran while one was open for 2% -> 4% of each run, Pallas kernels for 0% -> 0%
where the time goes in v1:
time: 281 us
  local copies, waits for them, and re-layouts  108 us (38%)
  blocking collectives  74.8 us (27%)
  starting transfers between devices  42.9 us (15%)
  other arithmetic  33.4 us (12%)
  waiting for transfers between devices  13.4 us (5%)
  matrix products  6.17 us (2%)
    scatter x1, local copies, waits for them, and re-layouts, shards(): jnp.zeros((3, capacity), jnp.float32).at[:, placed]  80.8 us
    psum x1, blocking collectives, shards(): gram, projection = lax.psum((gram_local, projection_local), ('gx', 'gy'))  74.8 us
    all_to_all x1, starting transfers between devices, tiled_gather(): return lax.all_to_all(copies, axis, dim, dim, tiled=True)  17.6 us
    ppermute x4, starting transfers between devices, extended(): lax.ppermute(tail, axis, [(i, (i + 1) % count) for i in range(ends)])  14.2 us
    unnamed x56, local copies, waits for them, and re-layouts  12.8 us
    div x2, other arithmetic, sweep_once(): return (divergence + stencil_sum(padded)) / (6.0 + diagonal)  12.2 us
    ppermute x4, starting transfers between devices, extended(): lax.ppermute(head, axis, [((i + 1) % count, i) for i in range(ends)])  11.2 us
    all_to_all x1, local copies, waits for them, and re-layouts, tiled_gather(): return lax.all_to_all(copies, axis, dim, dim, tiled=True)  9.07 us
  transfers between devices with their start and end apart: 9, of which 6 were waited for; matrix products, arithmetic and copies ran while one was open for 4% of the time, Pallas kernels for 0%

profile of v1, /device:TPU:1, one launch (start us, length us, event | category | flops | bytes accessed | tf_op | source)
XLA Modules:
  0.0 280.6 jit_solution(15479778463238182518)
XLA Ops:
  0.6 0.0 copy-start
  0.6 0.9 fusion.35
  1.6 5.1 %collective-permute-start = (f32[1,16,512]{2,0,1:T(1,128)S(1)}, f32[1,16,512]{2,0,1:T(1,128)S(1)}, u32[]{:S(2)}, u32[]{:S(2)}) collective-permute-start(f32[1,16,512]{2,0,1:T(1,128)S(1)} %copy.38), channel_id=1, source_target_pairs={{32,0},{64,32},{96,64},{128,96},{160,128},{192,160},{224,192},{33,... | collective-permute-start | bytes 98312 | tf_op jit(solution)/shard_map/ppermute | solution.py:24
  6.7 1.9 collective-permute-start.1
  8.6 2.8 %copy.39 = f32[64,16,512]{2,0,1:T(8,128)S(1)} copy(f32[64,16,512]{2,1,0:T(8,128)} %param.10) | data formatting | bytes 4194304 | tf_op args[0]
  11.5 0.0 collective-permute-done
  11.5 0.0 collective-permute-done.1
  11.5 1.3 collective-permute-start.2
  12.8 0.0 copy-start.3
  12.8 0.0 copy-start.5
  12.8 4.3 %collective-permute-start.3 = (f32[66,1,512]{2,0,1:T(8,128)S(1)}, f32[66,1,512]{2,0,1:T(8,128)S(1)}, u32[]{:S(2)}, u32[]{:S(2)}) collective-permute-start(f32[66,1,512]{2,0,1:T(8,128)S(1)} %get-tuple-element.16), channel_id=1, source_target_pairs={{0,1},{1,2},{2,3},{3,4},{4,5},{5,6},{6,7},{7,8},{8,9},{9,10},{10,1... | collective-permute-start | bytes 405512 | tf_op jit(solution)/shard_map/ppermute | solution.py:22
  17.1 1.2 collective-permute-done.2
  18.3 1.2 collective-permute-done.3
  19.5 2.8 %select_maximum_fusion.4 = f32[66,18,514]{2,0,1:T(8,128)S(1)} fusion(f32[66,1,512]{2,0,1:T(8,128)S(1)} %collective-permute-done.2, f32[66,1,512]{2,0,1:T(8,128)S(1)} %collective-permute-done.3, f32[1,16,512]{2,0,1:T(1,128)S(1)} %collective-permute-done, f32[64,16,512]{2,0,1:T(8,128)S(1)} %copy.39, f32[1,16,512]{2,0,1:T(1,128)S(1)} %collective-permute-done.1), kind=kLoop, calls=%fused_computation.7 | loop fusion | flops 7327584 | bytes 4875552 | tf_op jit(solution)/shard_map/concatenate | solution.py:20
  22.4 0.0 copy-done.3
  22.4 0.0 copy-done.5
  22.4 6.8 %fusion.7 = f32[64,16,512]{2,0,1:T(8,128)S(1)} fusion(f32[66,18,514]{2,0,1:T(8,128)S(1)} %select_maximum_fusion.4, f32[66,1,512]{2,0,1:T(8,128)S(1)} %collective-permute-done.3, f32[1,16,512]{2,0,1:T(1,128)S(1)} %collective-permute-done, f32[64,16,512]{2,0,1:T(8,128)S(1)} %copy.39, f32[1,16,512]{2,0,1:T(1,128)S(1)} %collective-permute-done.1, ...), kind=kLoop, calls=%fused_computation.29 | loop fusion | flops 8388608 | bytes 12918784 | tf_op jit(solution)/shard_map/div | solution.py:41
  29.2 0.1 fusion.34
  29.3 3.5 %collective-permute-start.4 = (f32[1,16,512]{2,0,1:T(1,128)S(1)}, f32[1,16,512]{2,0,1:T(1,128)S(1)}, u32[]{:S(2)}, u32[]{:S(2)}) collective-permute-start(f32[1,16,512]{2,0,1:T(1,128)S(1)} %get-tuple-element.19), channel_id=1, source_target_pairs={{32,0},{64,32},{96,64},{128,96},{160,128},{192,160},{224,192},{33,... | collective-permute-start | bytes 98312 | tf_op jit(solution)/shard_map/ppermute | solution.py:24
  32.8 2.6 collective-permute-start.5
  35.4 0.0 collective-permute-done.4
  35.4 1.0 collective-permute-done.5
  36.4 0.7 pad_maximum_fusion.16
  37.1 1.3 collective-permute-start.6
  38.4 5.4 %collective-permute-start.7 = (f32[66,1,512]{2,0,1:T(8,128)}, f32[66,1,512]{2,0,1:T(8,128)}, u32[]{:S(2)}, u32[]{:S(2)}) collective-permute-start(f32[66,1,512]{2,0,1:T(8,128)} %get-tuple-element.14), channel_id=1, source_target_pairs={{0,1},{1,2},{2,3},{3,4},{4,5},{5,6},{6,7},{7,8},{8,9},{9,10},{10,1... | collective-permute-start | bytes 405512 | tf_op jit(solution)/shard_map/ppermute | solution.py:22
  43.8 1.7 collective-permute-done.6
  45.6 1.4 collective-permute-done.7
  47.0 3.6 %select_maximum_fusion = f32[66,18,514]{2,0,1:T(8,128)S(1)} fusion(f32[66,1,512]{2,0,1:T(8,128)S(1)} %collective-permute-done.6, f32[66,1,512]{2,0,1:T(8,128)} %collective-permute-done.7, f32[1,16,512]{2,0,1:T(1,128)S(1)} %collective-permute-done.4, f32[64,16,512]{2,0,1:T(8,128)S(1)} %fusion.7, f32[1,16,512]{2,0,1:T(1,128)S(1)} %collective-permute-done.5), kind=kLoop, calls=%fused_computation.3 | loop fusion | flops 7327584 | bytes 4875552 | tf_op jit(solution)/shard_map/concatenate | solution.py:20
  50.6 0.0 copy-done.4
  50.6 0.0 copy-done.6
  50.6 0.0 copy-start.9
  50.7 0.0 copy-start.10
  50.7 5.4 %fusion.2 = f32[64,16,512]{2,0,1:T(8,128)S(1)} fusion(f32[66,18,514]{2,0,1:T(8,128)S(1)} %select_maximum_fusion, f32[66,1,512]{2,0,1:T(8,128)} %collective-permute-done.7, f32[1,16,512]{2,0,1:T(1,128)S(1)} %collective-permute-done.4, f32[64,16,512]{2,0,1:T(8,128)S(1)} %fusion.7, f32[1,16,512]{2,0,1:T(1,128)S(1)} %collective-permute-done.5, ...), kind=kLoop, calls=%fused_computation.14 | loop fusion | flops 8388608 | bytes 12918784 | tf_op jit(solution)/shard_map/div | solution.py:41
  56.0 0.0 copy-start.1
  56.0 1.3 copy-done.1
  57.4 0.2 slice.128
  57.6 0.5 copy.46
  58.0 0.1 mul.33
  58.1 0.0 copy-done.10
  58.6 0.0 copy-start.2
  58.7 0.8 copy-done.7
  59.5 17.6 %all-to-all-start = ((f32[3,32,1024]{2,0,1:T(4,128)}), f32[3,32,1024]{2,0,1:T(4,128)}, u32[]{:S(2)}, u32[]{:S(2)}) async-start(f32[3,32,1024]{2,0,1:T(4,128)} %bitcast.80), calls=%async_computation | async-start | bytes 1048576 | tf_op jit(solution)/shard_map/all_to_all | solution.py:11
  77.0 1.2 compare_select_fusion
  78.9 2.5 copy.50
  81.3 2.9 %convolution_bitcast_fusion = f32[32,32]{0,1:T(8,128)S(1)} fusion(f32[32,3,3072]{2,0,1:T(8,128)} %param.18, f32[3072]{0:T(1024)S(1)} %fusion.32), kind=kOutput, calls=%fused_computation.49 | convolution fusion | flops 113541120 | bytes 1196032 | tf_op jit(solution)/shard_map/dot_general | solution.py:52
  84.3 2.5 copy.52
  86.8 6.9 %all-to-all-done = f32[3,32,1024]{2,0,1:T(4,128)} async-done(((f32[3,32,1024]{2,0,1:T(4,128)}), f32[3,32,1024]{2,0,1:T(4,128)}, u32[]{:S(2)}, u32[]{:S(2)}) %all-to-all-start) | async-done | bytes 393248 | tf_op jit(solution)/shard_map/all_to_all | solution.py:11
  93.7 9.1 %copy.47 = f32[32768,3]{1,0:T(8,128)} copy(f32[32768,3]{0,1:T(4,128)} %bitcast.7) | data formatting | bytes 786432 | tf_op jit(solution)/shard_map/all_to_all | solution.py:11
  102.7 80.8 %scatter_custom_fusion = f32[3,3072]{0,1:T(8,128)S(1)} fusion(s32[32768]{0:T(1024)S(1)} %bitcast.81, f32[32768,3]{1,0:T(8,128)} %copy.47, f32[]{:T(128)} %constant.70.clone.1), kind=kCustom, calls=%fused_computation.58 | custom fusion | bytes 37376 | tf_op jit(solution)/shard_map/scatter | solution.py:62
  183.6 3.1 %multiply_bitcast_fusion = f32[3,3072,1]{0,1,2:T(8,128)} fusion(f32[3,3072]{0,1:T(8,128)S(1)} %scatter_custom_fusion, f32[3,3072]{0,1:T(8,128)} %copy.50, f32[3072]{0:T(1024)S(1)} %fusion.32), kind=kLoop, calls=%fused_computation.45 | loop fusion | flops 18432 | bytes 122880 | tf_op jit(solution)/shard_map/mul | solution.py:63
  186.6 1.9 copy.55
  188.5 2.3 fusion.20
  190.8 74.8 %all-reduce.2 = (f32[32,32]{0,1:T(8,128)S(1)}, f32[32]{0:T(128)S(1)}) all-reduce(f32[32,32]{0,1:T(8,128)S(1)} %convolution_bitcast_fusion, f32[32]{0:T(128)S(1)} %fusion.20), channel_id=1, replica_groups=mesh['gx'=8,'gy'=32] {'gx','gy'}, use_global_device_ids=true, to_apply=%region_1.2 | all-reduce | flops 1056 | bytes 8448 | tf_op jit(solution)/shard_map/psum | solution.py:67
  265.6 0.1 copy.49
  265.7 2.9 %cholesky.16 = f32[32,32]{1,0:T(8,128)S(1)} custom-call(f32[32,32]{1,0:T(8,128)S(1)} %fusion.31), custom_call_target="Cholesky" | custom-call | tf_op jit(solution)/shard_map/jit(cholesky)/cholesky | solution.py:68
  268.6 0.6 compare_reduce_fusion
  269.2 0.7 fusion.28
  269.9 2.4 custom-call.10
  272.3 0.2 convolution_bitcast_fusion.2
  272.5 0.1 fusion.19
  272.6 0.7 fusion.12
  273.3 1.7 copy.57
  275.0 3.1 %fusion.11 = f32[3,3072]{0,1:T(8,128)} fusion(f32[3,3072]{0,1:T(8,128)S(1)} %scatter_custom_fusion, f32[1,3,3072]{1,2,0:T(8,128)} %copy.57, f32[3072]{0:T(1024)S(1)} %fusion.32), kind=kLoop, calls=%fused_computation.44 | loop fusion | flops 18432 | bytes 122880 | tf_op jit(solution)/shard_map/mul | solution.py:73
  278.1 2.5 copy.53
  (46 shorter events, 0.5 us)
Async XLA Ops:
  0.6 272.0 %copy-start = (f32[32,3,3072]{2,0,1:T(8,128)S(1)}, f32[32,3,3072]{2,0,1:T(8,128)}, u32[]{:S(2)}) copy-start(f32[32,3,3072]{2,0,1:T(8,128)} %param.19) | copy-start | bytes 3538948
  1.6 9.9 %collective-permute-start = (f32[1,16,512]{2,0,1:T(1,128)S(1)}, f32[1,16,512]{2,0,1:T(1,128)S(1)}, u32[]{:S(2)}, u32[]{:S(2)}) collective-permute-start(f32[1,16,512]{2,0,1:T(1,128)S(1)} %copy.38), channel_id=1, source_target_pairs={{32,0},{64,32},{96,64},{128,96},{160,128},{192,160},{224,192},{33,... | collective-permute-start | bytes 98312 | tf_op jit(solution)/shard_map/ppermute | solution.py:24
  6.7 4.8 %collective-permute-start.1 = (f32[1,16,512]{2,0,1:T(1,128)S(1)}, f32[1,16,512]{2,0,1:T(1,128)S(1)}, u32[]{:S(2)}, u32[]{:S(2)}) collective-permute-start(f32[1,16,512]{2,0,1:T(1,128)S(1)} %copy.40), channel_id=1, source_target_pairs={{0,32},{32,64},{64,96},{96,128},{128,160},{160,192},{192,224},{1,3... | collective-permute-start | bytes 98312 | tf_op jit(solution)/shard_map/ppermute | solution.py:22
  11.5 6.8 %collective-permute-start.2 = (f32[66,1,512]{2,0,1:T(8,128)S(1)}, f32[66,1,512]{2,0,1:T(8,128)S(1)}, u32[]{:S(2)}, u32[]{:S(2)}) collective-permute-start(f32[66,1,512]{2,0,1:T(8,128)S(1)} %get-tuple-element.17), channel_id=1, source_target_pairs={{1,0},{2,1},{3,2},{4,3},{5,4},{6,5},{7,6},{8,7},{9,8},{10,9},{11,1... | collective-permute-start | bytes 405512 | tf_op jit(solution)/shard_map/ppermute | solution.py:24
  12.8 9.5 %copy-start.3 = (f32[64,16,512]{2,1,0:T(8,128)S(1)}, f32[64,16,512]{2,1,0:T(8,128)}, u32[]{:S(2)}) copy-start(f32[64,16,512]{2,1,0:T(8,128)} %param.11) | copy-start | bytes 6291460
  12.8 9.5 %copy-start.5 = (f32[64,16,512]{2,1,0:T(8,128)S(1)}, f32[64,16,512]{2,1,0:T(8,128)}, u32[]{:S(2)}) copy-start(f32[64,16,512]{2,1,0:T(8,128)} %param.12) | copy-start | bytes 6291460
  12.8 6.7 %collective-permute-start.3 = (f32[66,1,512]{2,0,1:T(8,128)S(1)}, f32[66,1,512]{2,0,1:T(8,128)S(1)}, u32[]{:S(2)}, u32[]{:S(2)}) collective-permute-start(f32[66,1,512]{2,0,1:T(8,128)S(1)} %get-tuple-element.16), channel_id=1, source_target_pairs={{0,1},{1,2},{2,3},{3,4},{4,5},{5,6},{6,7},{7,8},{8,9},{9,10},{10,1... | collective-permute-start | bytes 405512 | tf_op jit(solution)/shard_map/ppermute | solution.py:22
  29.3 6.1 %collective-permute-start.4 = (f32[1,16,512]{2,0,1:T(1,128)S(1)}, f32[1,16,512]{2,0,1:T(1,128)S(1)}, u32[]{:S(2)}, u32[]{:S(2)}) collective-permute-start(f32[1,16,512]{2,0,1:T(1,128)S(1)} %get-tuple-element.19), channel_id=1, source_target_pairs={{32,0},{64,32},{96,64},{128,96},{160,128},{192,160},{224,192},{33,... | collective-permute-start | bytes 98312 | tf_op jit(solution)/shard_map/ppermute | solution.py:24
  32.8 3.6 %collective-permute-start.5 = (f32[1,16,512]{2,0,1:T(1,128)S(1)}, f32[1,16,512]{2,0,1:T(1,128)S(1)}, u32[]{:S(2)}, u32[]{:S(2)}) collective-permute-start(f32[1,16,512]{2,0,1:T(1,128)S(1)} %get-tuple-element.18), channel_id=1, source_target_pairs={{0,32},{32,64},{64,96},{96,128},{128,160},{160,192},{192,224},{1,3... | collective-permute-start | bytes 98312 | tf_op jit(solution)/shard_map/ppermute | solution.py:22
  37.1 8.4 %collective-permute-start.6 = (f32[66,1,512]{2,0,1:T(8,128)}, f32[66,1,512]{2,0,1:T(8,128)S(1)}, u32[]{:S(2)}, u32[]{:S(2)}) collective-permute-start(f32[66,1,512]{2,0,1:T(8,128)} %get-tuple-element.15), channel_id=1, source_target_pairs={{1,0},{2,1},{3,2},{4,3},{5,4},{6,5},{7,6},{8,7},{9,8},{10,9},{11,1... | collective-permute-start | bytes 405512 | tf_op jit(solution)/shard_map/ppermute | solution.py:24
  38.4 8.6 %collective-permute-start.7 = (f32[66,1,512]{2,0,1:T(8,128)}, f32[66,1,512]{2,0,1:T(8,128)}, u32[]{:S(2)}, u32[]{:S(2)}) collective-permute-start(f32[66,1,512]{2,0,1:T(8,128)} %get-tuple-element.14), channel_id=1, source_target_pairs={{0,1},{1,2},{2,3},{3,4},{4,5},{5,6},{6,7},{7,8},{8,9},{9,10},{10,1... | collective-permute-start | bytes 405512 | tf_op jit(solution)/shard_map/ppermute | solution.py:22
  43.8 6.8 %copy-start.4 = (f32[64,16,512]{2,1,0:T(8,128)S(1)}, f32[64,16,512]{2,1,0:T(8,128)}, u32[]{:S(2)}) copy-start(f32[64,16,512]{2,1,0:T(8,128)} %param.11) | copy-start | bytes 6291460
  43.8 6.8 %copy-start.6 = (f32[64,16,512]{2,1,0:T(8,128)S(1)}, f32[64,16,512]{2,1,0:T(8,128)}, u32[]{:S(2)}) copy-start(f32[64,16,512]{2,1,0:T(8,128)} %param.12) | copy-start | bytes 6291460
  50.6 7.5 %copy-start.9 = (f32[3,1024]{1,0:T(4,128)S(1)}, f32[3,1024]{1,0:T(4,128)}, u32[]{:S(2)}) copy-start(f32[3,1024]{1,0:T(4,128)} %param.14) | copy-start | bytes 36868
  50.7 7.5 %copy-start.10 = (f32[3,1024]{1,0:T(4,128)S(1)}, f32[3,1024]{1,0:T(4,128)}, u32[]{:S(2)}) copy-start(f32[3,1024]{1,0:T(4,128)} %param.13) | copy-start | bytes 36868
  56.0 1.3 copy-start.1
  57.4 19.7 %copy-start.8 = (s32[1,32768]{1,0:T(1,128)S(1)}, s32[1,32768]{1,0:T(1,128)}, u32[]{:S(2)}) copy-start(s32[1,32768]{1,0:T(1,128)} %param.15) | copy-start | bytes 393220
  58.6 25.6 %copy-start.2 = (f32[64,16,512]{2,0,1:T(8,128)S(1)}, f32[64,16,512]{2,0,1:T(8,128)}, u32[]{:S(2)}) copy-start(f32[64,16,512]{2,0,1:T(8,128)} %copy-done.1) | copy-start | bytes 6291460
  58.7 0.8 copy-start.7
  59.5 34.2 %all-to-all-start = ((f32[3,32,1024]{2,0,1:T(4,128)}), f32[3,32,1024]{2,0,1:T(4,128)}, u32[]{:S(2)}, u32[]{:S(2)}) async-start(f32[3,32,1024]{2,0,1:T(4,128)} %bitcast.80), calls=%async_computation | async-start | bytes 1048576 | tf_op jit(solution)/shard_map/all_to_all | solution.py:11
